TPU v7x, 32 devices: a whole 2x2x4 slice. The times are simulated.
32 devices in a mesh: groups: 2 (over y), tp: 4 (over x, core), sp: 4 (over z).
Axes of the slice: x: 2, y: 2, z: 4, core: 2. Of those that a mesh axis runs over, the one named last changes fastest.
Arguments:
- query_rows: bfloat16 [4, 128, 4096], P('groups', ('sp', 'tp')), parts along dimension 0, may hold values from -100 to 100
- key_rows: bfloat16 [4, 128, 4096], P('groups', ('sp', 'tp')), parts along dimension 0, may hold values from -4 to 4
- value_rows: bfloat16 [4, 128, 4096], P('groups', ('sp', 'tp')), parts along dimension 0, may hold values from -6 to 6
- residual: bfloat16 [4, 128, 2560], P('groups', 'sp', 'tp'), parts along dimension 0, may hold values from -100 to 100
- modulation: float32 [4, 2560], P(None, 'tp'), may hold values from -3 to 3
- out_weight: bfloat16 [2560, 4096], P('tp', 'sp'), may hold values from -0.375 to 0.375
- up_weight: bfloat16 [2560, 7168], P('sp', 'tp'), may hold values from -0.125 to 0.125
- down_weight: bfloat16 [2560, 7168], P('sp', 'tp'), may hold values from -0.0625 to 0.0625
Outputs:
- block_out: bfloat16 [4, 128, 2560], P('groups', 'sp', 'tp'), parts along dimension 0
There are 2 independent parts, one for each index of `groups`. A program takes and returns all parts, laid end to end along the dimension named above; an argument that names none is the same for every part. Nothing has to cross between parts.
All inputs are finite; a program needn't handle non-finite values.
Results may differ from a plain program's by a relative error of at most 0.0044.
Values may be sent and summed in bfloat16 or wider, within the bound.
A program may use at most 64 MiB of HBM per device.

v0:
```python
import math
import jax
import jax.numpy as jnp
from jax import lax
from jax.sharding import PartitionSpec as P

D = 2560
HEAD_FEATURES = 128


def contract_last(left, right):
    return lax.dot_general(
        left, right, (((1,), (1,)), ((), ())), preferred_element_type=jnp.float32
    )


def attend(query_part, key_part, value_part):
    query_heads, key_heads, value_heads = (
        lax.all_to_all(query_part, "sp", split_axis=2, concat_axis=1, tiled=True),
        lax.all_to_all(key_part, "sp", split_axis=2, concat_axis=1, tiled=True),
        lax.all_to_all(value_part, "sp", split_axis=2, concat_axis=1, tiled=True),
    )
    batches, query_count, local_width = query_heads.shape
    local_heads = local_width // HEAD_FEATURES
    grouped = query_heads.reshape(batches, query_count, local_heads, HEAD_FEATURES)
    score_scale = 1.0 / math.sqrt(HEAD_FEATURES)

    def absorb_block(running, blocks):
        block_keys, block_values = blocks
        highest, row_total, weighted_values = running
        attention_logits = (
            jnp.einsum("bqhd,bkhd->bqhk", grouped, block_keys, preferred_element_type=jnp.float32)
            * score_scale
        )
        raised = jnp.maximum(highest, jnp.max(attention_logits, axis=-1))
        damping = jnp.exp(highest - raised)
        exponent = jnp.exp(attention_logits - raised[..., None])
        row_total = row_total * damping + jnp.sum(exponent, axis=-1)
        weighted_values = weighted_values * damping[..., None] + jnp.einsum(
            "bqhk,bkhd->bqhd",
            exponent.astype(jnp.bfloat16),
            block_values,
            preferred_element_type=jnp.float32,
        )
        return (raised, row_total, weighted_values)

    def scan_step(running, blocks):
        return (absorb_block(running, blocks), None)

    def absorb(running, section):
        key_section, value_section = section
        key_count = key_section.shape[1]
        shaped_keys = key_section.reshape(batches, key_count, local_heads, HEAD_FEATURES)
        shaped_values = value_section.reshape(batches, key_count, local_heads, HEAD_FEATURES)
        if key_count > 512 and key_count % 512 == 0:
            block_count = key_count // 512
            key_blocks = jnp.moveaxis(
                shaped_keys.reshape(batches, block_count, 512, local_heads, HEAD_FEATURES), 1, 0
            )
            value_blocks = jnp.moveaxis(
                shaped_values.reshape(batches, block_count, 512, local_heads, HEAD_FEATURES), 1, 0
            )
            running, unused = lax.scan(scan_step, running, (key_blocks, value_blocks))
            return running
        return absorb_block(running, (shaped_keys, shaped_values))

    starting = (
        jnp.full((batches, query_count, local_heads), -jnp.inf, jnp.float32),
        jnp.zeros((batches, query_count, local_heads), jnp.float32),
        jnp.zeros((batches, query_count, local_heads, HEAD_FEATURES), jnp.float32),
    )
    highest, row_total, weighted_values = absorb(
        starting,
        (
            lax.all_gather(key_heads, "tp", axis=1, tiled=True),
            lax.all_gather(value_heads, "tp", axis=1, tiled=True),
        ),
    )
    normalized = (weighted_values / row_total[..., None]).astype(jnp.bfloat16)
    ordered = normalized.reshape(batches, query_count, local_width)
    return lax.all_to_all(ordered, "sp", split_axis=1, concat_axis=2, tiled=True)


def body(
    query_rows, key_rows, value_rows, residual, modulation, out_weight, up_weight, down_weight
):
    attended = attend(query_rows, key_rows, value_rows)
    stripes = lax.all_gather(attended, "tp", axis=1, tiled=True)
    batches, rows_block, inner_width = stripes.shape
    row_count = batches * rows_block
    flat_rows = stripes.reshape(row_count, inner_width)
    local_width = out_weight.shape[0]
    columns = flat_rows
    projected = contract_last(columns, lax.all_gather(out_weight, "sp", axis=1, tiled=True))
    mixed_rows = (
        residual.reshape(row_count, local_width).astype(jnp.float32) + modulation[0] * projected
    )
    first_sum, second_sum = lax.psum(
        (jnp.sum(mixed_rows, axis=1), jnp.sum(mixed_rows * mixed_rows, axis=1)), "tp"
    )
    row_mean = first_sum / D
    spread = second_sum / D - row_mean * row_mean
    normed = (
        (mixed_rows - row_mean[:, None])
        * lax.rsqrt(spread[:, None] + 1e-06)
        * (1.0 + modulation[2])
        + modulation[1]
    ).astype(jnp.bfloat16)
    gathered = lax.all_gather(normed, "tp", axis=1, tiled=True)
    columns = gathered
    hidden = jnp.dot(
        columns,
        lax.all_gather(up_weight, "sp", axis=0, tiled=True),
        preferred_element_type=jnp.float32,
    )
    active = jax.nn.gelu(hidden, approximate=True).astype(jnp.bfloat16)
    partial_out = contract_last(active, lax.all_gather(down_weight, "sp", axis=0, tiled=True))
    summed = lax.psum_scatter(
        partial_out.astype(jnp.bfloat16), "tp", scatter_dimension=1, tiled=True
    ).astype(jnp.float32)
    result = (mixed_rows + modulation[3] * summed).astype(jnp.bfloat16)
    return result.reshape(batches, rows_block, local_width)


def stationary(
    query_rows, key_rows, value_rows, residual, modulation, out_weight, up_weight, down_weight
):
    both = ("sp", "tp")
    stacked = jnp.stack((query_rows, key_rows, value_rows))
    mine = lax.all_to_all(stacked, both, split_axis=3, concat_axis=2, tiled=True)
    batches, tokens, width = mine.shape[1:]
    local_heads = width // HEAD_FEATURES
    heads = mine.reshape(3, batches, tokens, local_heads, HEAD_FEATURES)
    scores = jnp.einsum(
        "bqhd,bkhd->bhqk", heads[0], heads[1], preferred_element_type=jnp.float32
    ) * (1.0 / math.sqrt(HEAD_FEATURES))
    exponent = jnp.exp(scores - jnp.max(scores, axis=-1, keepdims=True))
    row_total = jnp.sum(exponent, axis=-1)
    weighted = jnp.einsum(
        "bhqk,bkhd->bqhd",
        exponent.astype(jnp.bfloat16),
        heads[2],
        preferred_element_type=jnp.float32,
    )
    attended = (weighted / jnp.swapaxes(row_total, 1, 2)[..., None]).astype(jnp.bfloat16)
    attended = attended.reshape(batches, tokens, width)
    attended = lax.all_gather(attended, "tp", axis=2, tiled=True)
    row_count = batches * tokens
    partial = contract_last(attended.reshape(row_count, -1), out_weight)
    partial = partial.astype(jnp.bfloat16).reshape(batches, tokens, -1)
    projected = lax.psum_scatter(partial, "sp", scatter_dimension=1, tiled=True)
    mixed = residual.astype(jnp.float32) + modulation[0] * projected.astype(jnp.float32)
    first_sum, second_sum = lax.psum((jnp.sum(mixed, axis=2), jnp.sum(mixed * mixed, axis=2)), "tp")
    row_mean = first_sum / D
    spread = second_sum / D - row_mean * row_mean
    normed = (
        (mixed - row_mean[..., None]) * lax.rsqrt(spread[..., None] + 1e-06) * (1.0 + modulation[2])
        + modulation[1]
    ).astype(jnp.bfloat16)
    normed = lax.all_gather(normed, "tp", axis=2, tiled=True)
    normed = lax.all_to_all(normed, "sp", split_axis=2, concat_axis=1, tiled=True)
    hidden = jnp.dot(normed.reshape(row_count, -1), up_weight, preferred_element_type=jnp.float32)
    hidden = hidden.astype(jnp.bfloat16).reshape(batches, tokens, -1)
    hidden = lax.psum_scatter(hidden, "sp", scatter_dimension=1, tiled=True)
    active = jax.nn.gelu(hidden.astype(jnp.float32), approximate=True).astype(jnp.bfloat16)
    active = lax.all_gather(active, "sp", axis=1, tiled=True)
    down = contract_last(active.reshape(row_count, -1), down_weight)
    down = down.astype(jnp.bfloat16).reshape(batches, tokens, -1)
    down = lax.psum_scatter(down, "tp", scatter_dimension=1, tiled=True)
    size = lax.axis_size("tp")
    swap = [(s * size + t, t * size + s) for s in range(size) for t in range(size)]
    down = lax.ppermute(down, ("tp", "sp"), swap)
    return (mixed + modulation[3] * down.astype(jnp.float32)).astype(jnp.bfloat16)


def solution(mesh):
    in_specs = (
        P("groups", ("sp", "tp"), None),
        P("groups", ("sp", "tp"), None),
        P("groups", ("sp", "tp"), None),
        P("groups", "sp", "tp"),
        P(None, "tp"),
        P("tp", "sp"),
        P("sp", "tp"),
        P("sp", "tp"),
    )
    out_specs = P("groups", "sp", "tp")

    def block(*operands):
        sizes = mesh.shape
        rows = operands[0].shape[0] * operands[0].shape[1] * sizes["sp"] * sizes["tp"]
        square = sizes["sp"] == sizes["tp"]
        whole_heads = operands[0].shape[2] % (sizes["sp"] * sizes["tp"] * HEAD_FEATURES) == 0
        few = rows < operands[6].shape[0]
        return (stationary if square and whole_heads and few else body)(*operands)

    return jax.shard_map(block, mesh=mesh, in_specs=in_specs, out_specs=out_specs, check_vma=False)
```

profile of v0, /device:TPU:2, one launch (start us, length us, event | category | flops | bytes accessed | tf_op | source)
XLA Modules:
  0.0 260.4 jit_solution(14532735664056187032)
XLA Ops:
  6.5 1.2 pad_maximum_fusion
  7.8 10.7 %copy.54 = bf16[3,2,8,4096]{2,1,0,3:T(2,128)(2,1)} copy(bf16[3,2,8,4096]{3,2,1,0:T(8,128)(2,1)S(1)} %pad_maximum_fusion) | data formatting | bytes 786432 | tf_op jit(solution)/shard_map/stack | solution.py:129
  18.5 17.7 %reshape.59 = bf16[16,2,6144]{2,1,0:T(2,128)(2,1)S(1)} reshape(bf16[4096,3,2,8]{3,2,1,0:T(2,128)(2,1)} %bitcast.39) | data formatting | bytes 786432
  36.2 16.5 %all_to_all.30 = bf16[16,2,6144]{2,1,0:T(2,128)(2,1)S(1)} all-to-all(bf16[16,2,6144]{2,1,0:T(2,128)(2,1)S(1)} %reshape.59), channel_id=1, replica_groups=mesh['groups'=2,'tp'=4,'sp'=4] {'sp','tp'}, dimensions={0} | all-to-all | bytes 786432 | tf_op jit(solution)/shard_map/all_to_all | solution.py:130
  52.7 8.3 %reshape.60 = bf16[4096,3,2,8]{3,2,1,0:T(2,128)(2,1)} reshape(bf16[16,2,6144]{2,1,0:T(2,128)(2,1)S(1)} %all_to_all.30) | data formatting | bytes 786432
  61.0 13.3 %copy.55 = bf16[3,2,8,16,256]{4,2,3,1,0:T(8,128)(2,1)S(1)} copy(bf16[3,2,8,16,256]{2,1,0,4,3:T(2,128)(2,1)} %bitcast.40) | data formatting | bytes 786432 | tf_op jit(solution)/shard_map/all_to_all | solution.py:130
  75.1 7.9 %all_gather.9 = bf16[2,128,1024]{2,1,0:T(8,128)(2,1)S(1)} all-gather(bf16[2,128,256]{2,1,0:T(8,128)(2,1)S(1)} %copy.60), channel_id=1, replica_groups=mesh['groups'=2,'tp'=4,'sp'=4] {'tp'}, dimensions={2}, use_global_device_ids=true | all-gather | bytes 655360 | tf_op jit(solution)/shard_map/all_gather | solution.py:147
  83.0 1.9 convolution_convert_fusion.2
  87.4 34.9 %all-reduce.6.cloned.1.call-done = bf16[2,128,640]{2,0,1:T(2,128)(2,1)} async-done(((bf16[2,128,640]{2,0,1:T(2,128)(2,1)}), bf16[2,128,640]{2,0,1:T(2,128)(2,1)}) %all-reduce.6.cloned.1.call-update) | async-done | bytes 327696
  123.3 5.9 %all-reduce.2 = (f32[2,32]{1,0:T(2,128)S(1)}, f32[2,32]{1,0:T(2,128)S(1)}) all-reduce(f32[2,32]{1,0:T(2,128)S(1)} %get-tuple-element.6, f32[2,32]{1,0:T(2,128)S(1)} %get-tuple-element.5), channel_id=1, replica_groups=mesh['groups'=2,'tp'=4,'sp'=4] {'tp'}, use_global_device_ids=true, to_apply=%region_6.0 | all-reduce | flops 128 | bytes 1024 | tf_op jit(solution)/shard_map/psum | solution.py:153
  129.4 6.0 %all_gather.10 = bf16[2,32,2560]{2,1,0:T(8,128)(2,1)S(1)} all-gather(bf16[2,32,640]{2,1,0:T(8,128)(2,1)S(1)} %add_convert_fusion.1), channel_id=1, replica_groups=mesh['groups'=2,'tp'=4,'sp'=4] {'tp'}, dimensions={2}, use_global_device_ids=true | all-gather | bytes 409600 | tf_op jit(solution)/shard_map/all_gather | solution.py:160
  135.3 2.2 copy.63
  137.5 3.7 %reshape.61 = bf16[4,2,20480]{2,1,0:T(2,128)(2,1)S(1)} reshape(bf16[2560,2,32]{2,1,0:T(2,128)(2,1)} %bitcast.41) | data formatting | bytes 655360
  141.2 14.0 %all_to_all.31 = bf16[4,2,20480]{2,1,0:T(2,128)(2,1)S(1)} all-to-all(bf16[4,2,20480]{2,1,0:T(2,128)(2,1)S(1)} %reshape.61), channel_id=1, replica_groups=mesh['groups'=2,'tp'=4,'sp'=4] {'sp'}, dimensions={0} | all-to-all | bytes 655360 | tf_op jit(solution)/shard_map/all_to_all | solution.py:161
  155.2 1.7 reshape.62
  156.9 3.5 %copy.69 = bf16[2,32,4,640]{3,2,1,0:T(4,128)(2,1)S(1)} copy(bf16[2,32,4,640]{1,0,3,2:T(2,128)(2,1)} %bitcast.42) | data formatting | bytes 655360 | tf_op jit(solution)/shard_map/all_to_all | solution.py:161
  160.5 1.8 convolution_convert_fusion
  162.4 24.5 %reduce-scatter.2.cloned.1.call-done = bf16[2,32,1792]{2,1,0:T(8,128)(2,1)} async-done(((bf16[2,128,1792]{2,1,0:T(8,128)(2,1)}), bf16[2,32,1792]{2,1,0:T(8,128)(2,1)}) %reduce-scatter.2.cloned.1.call-update) | async-done | bytes 229392 | tf_op jit(solution)/shard_map/reduce_scatter | solution.py:164
  186.8 1.1 fusion.7
  187.9 19.0 %all_gather.11 = bf16[2,128,1792]{2,1,0:T(8,128)(2,1)S(1)} all-gather(bf16[2,32,1792]{2,1,0:T(8,128)(2,1)S(1)} %fusion.7), channel_id=1, replica_groups=mesh['groups'=2,'tp'=4,'sp'=4] {'sp'}, dimensions={1}, use_global_device_ids=true | all-gather | bytes 1146880 | tf_op jit(solution)/shard_map/all_gather | solution.py:166
  206.9 2.6 convolution_convert_fusion.1
  211.8 29.9 %all-reduce.8.cloned.1.call-done = bf16[2,128,640]{2,0,1:T(2,128)(2,1)} async-done(((bf16[2,128,640]{2,0,1:T(2,128)(2,1)}), bf16[2,128,640]{2,0,1:T(2,128)(2,1)}) %all-reduce.8.cloned.1.call-update) | async-done | bytes 327696
  242.7 5.8 %collective-permute-start = (bf16[2,32,640]{2,1,0:T(8,128)(2,1)S(1)}, bf16[2,32,640]{2,1,0:T(8,128)(2,1)S(1)}, u32[]{:S(2)}, u32[]{:S(2)}) collective-permute-start(bf16[2,32,640]{2,1,0:T(8,128)(2,1)S(1)} %copy.67), channel_id=1, source_target_pairs={{0,0},{1,4},{2,8},{3,12},{4,1},{5,5},{6,9},{7,13},{8,2},{9,6},{10,... | collective-permute-start | bytes 245768 | tf_op jit(solution)/shard_map/ppermute | solution.py:172
  248.5 4.7 %collective-permute-done = bf16[2,32,640]{2,1,0:T(8,128)(2,1)S(1)} collective-permute-done((bf16[2,32,640]{2,1,0:T(8,128)(2,1)S(1)}, bf16[2,32,640]{2,1,0:T(8,128)(2,1)S(1)}, u32[]{:S(2)}, u32[]{:S(2)}) %collective-permute-start) | collective-permute-done | bytes 81952 | tf_op jit(solution)/shard_map/ppermute | solution.py:172
  (37 shorter events, 7.1 us)
Async XLA Ops:
  6.5 153.9 %copy-start = (bf16[640,1792]{1,0:T(8,128)(2,1)S(1)}, bf16[640,1792]{1,0:T(8,128)(2,1)}, u32[]{:S(2)}) copy-start(bf16[640,1792]{1,0:T(8,128)(2,1)} %param.14) | copy-start | bytes 6881284
  6.5 115.7 %all-reduce.6.cloned.1.call-start = ((), (), s32[]{:S(2)}) async-start(), calls=%async_computation.4 | async-start | bytes 655360
  75.0 11.1 %copy-start.4 = (u32[32]{0:T(128)S(1)}, u32[32]{0:T(128)}, u32[]{:S(2)}) copy-start(u32[32]{0:T(128)} %constant.26) | copy-start | bytes 388
  75.0 12.3 %copy-start.2 = (f32[4,640]{1,0:T(4,128)S(1)}, f32[4,640]{1,0:T(4,128)}, u32[]{:S(2)}) copy-start(f32[4,640]{1,0:T(4,128)} %param.12) | copy-start | bytes 30724
  75.0 48.2 %copy-start.1 = (bf16[2,32,640]{2,1,0:T(8,128)(2,1)S(1)}, bf16[2,32,640]{2,1,0:T(8,128)(2,1)}, u32[]{:S(2)}) copy-start(bf16[2,32,640]{2,1,0:T(8,128)(2,1)} %param.11) | copy-start | bytes 245764
  86.0 100.8 %reduce-scatter.2.cloned.1.call-start = ((), (), s32[]{:S(2)}) async-start(), calls=%async_computation.3 | async-start | bytes 1146880 | tf_op jit(solution)/shard_map/reduce_scatter | solution.py:164
  162.3 79.4 %all-reduce.8.cloned.1.call-start = ((), (), s32[]{:S(2)}) async-start(), calls=%async_computation.5 | async-start | bytes 655360
  206.9 3.7 %copy-start.3 = (u32[32]{0:T(128)S(1)}, u32[32]{0:T(128)}, u32[]{:S(2)}) copy-start(u32[32]{0:T(128)} %constant.30) | copy-start | bytes 388
  242.7 10.5 %collective-permute-start = (bf16[2,32,640]{2,1,0:T(8,128)(2,1)S(1)}, bf16[2,32,640]{2,1,0:T(8,128)(2,1)S(1)}, u32[]{:S(2)}, u32[]{:S(2)}) collective-permute-start(bf16[2,32,640]{2,1,0:T(8,128)(2,1)S(1)} %copy.67), channel_id=1, source_target_pairs={{0,0},{1,4},{2,8},{3,12},{4,1},{5,5},{6,9},{7,13},{8,2},{9,6},{10,... | collective-permute-start | bytes 245768 | tf_op jit(solution)/shard_map/ppermute | solution.py:172
Sparse Core Ops, SparseCore 0:
  86.1 36.0 all-reduce.5
  162.5 24.3 reduce-scatter.1
  210.7 31.0 all-reduce.7
where the time goes:
time: 261 us; the launch traced here: 260 us
  waiting for transfers between devices  94 us (36%)
  blocking collectives  69.1 us (26%)
  local copies, waits for them, and re-layouts  66.7 us (26%)
  between operations  14.6 us (6%)
  matrix products  6.76 us (3%)
  starting transfers between devices  5.85 us (2%)
  other arithmetic  3.33 us (1%)
    unnamed x5, waiting for transfers between devices  64.9 us
    unnamed x18, local copies, waits for them, and re-layouts  34.6 us
    reduce_scatter x1, waiting for transfers between devices, stationary(): hidden = lax.psum_scatter(hidden, 'sp', scatter_dimension=1, tiled=True)  24.5 us
    all_gather x1, blocking collectives, stationary(): active = lax.all_gather(active, 'sp', axis=1, tiled=True)  19 us
    all_to_all x1, blocking collectives, stationary(): lax.all_to_all(stacked, both, split_axis=3, concat_axis=2, tiled=True)  16.5 us
    all_to_all x1, blocking collectives, stationary(): lax.all_to_all(normed, 'sp', split_axis=2, concat_axis=1, tiled=True)  14 us
    all_to_all x1, local copies, waits for them, and re-layouts, stationary(): lax.all_to_all(stacked, both, split_axis=3, concat_axis=2, tiled=True)  13.3 us
    another operation x1, local copies, waits for them, and re-layouts, stationary(): stacked = jnp.stack((query_rows, key_rows, value_rows))  10.7 us
  transfers between devices with their start and end apart: 4, of which 4 were waited for; matrix products, arithmetic and copies ran while one was open for 0% of the time, Pallas kernels for 0%

commit v1 on v0

--- a/solution.py
+++ b/solution.py
@@ -127,7 +127,16 @@
 ):
     both = ("sp", "tp")
     stacked = jnp.stack((query_rows, key_rows, value_rows))
-    mine = lax.all_to_all(stacked, both, split_axis=3, concat_axis=2, tiled=True)
+    number_the_halves = lambda x_in, device_axis: jnp.concatenate(
+        lax.all_to_all(
+            jnp.stack(jnp.split(x_in, lax.axis_size(device_axis), axis=3)),
+            axis_name=device_axis,
+            split_axis=0,
+            concat_axis=0,
+        ),
+        axis=2,
+    )
+    mine = number_the_halves(stacked, device_axis=both)
     batches, tokens, width = mine.shape[1:]
     local_heads = width // HEAD_FEATURES
     heads = mine.reshape(3, batches, tokens, local_heads, HEAD_FEATURES)

time: 261 us -> 211 us (0.81)
  local copies, waits for them, and re-layouts: 66.7 us -> 16.8 us
    unnamed x18 -> x31, local copies, waits for them, and re-layouts: 34.6 us -> 8.59 us
    all_to_all x1 -> x0, local copies, waits for them, and re-layouts: 13.3 us -> none  [stationary(): lax.all_to_all(stacked, both, split_axis=3, concat_axis=2, tiled=True)]
    another operation x1, local copies, waits for them, and re-layouts: 10.7 us -> 0.01 us  [stationary(): jnp.stack(jnp.split(x_in, lax.axis_size(device_axis), axis=3))]
  transfers between devices with their start and end apart: 4 -> 4, of which waited for: 4 -> 4; matrix products, arithmetic and copies ran while one was open for 0% -> 1% of each run, Pallas kernels for 0% -> 0%
where the time goes in v1:
time: 211 us
  waiting for transfers between devices  94 us (45%)
  blocking collectives  69.1 us (33%)
  local copies, waits for them, and re-layouts  16.8 us (8%)
  between operations  14.7 us (7%)
  matrix products  6.78 us (3%)
  starting transfers between devices  5.85 us (3%)
  other arithmetic  3.33 us (2%)
    unnamed x5, waiting for transfers between devices  64.9 us
    reduce_scatter x1, waiting for transfers between devices, stationary(): hidden = lax.psum_scatter(hidden, 'sp', scatter_dimension=1, tiled=True)  24.5 us
    all_gather x1, blocking collectives, stationary(): active = lax.all_gather(active, 'sp', axis=1, tiled=True)  18.9 us
    all_to_all x1, blocking collectives, stationary(): lax.all_to_all(jnp.stack(jnp.split(x_in, lax.axis_size(device_axis), axis...  16.5 us
    all_to_all x1, blocking collectives, stationary(): lax.all_to_all(normed, 'sp', split_axis=2, concat_axis=1, tiled=True)  14 us
    unnamed x31, local copies, waits for them, and re-layouts  8.59 us
    all_gather x1, blocking collectives, stationary(): attended = lax.all_gather(attended, 'tp', axis=2, tiled=True)  7.85 us
    all_gather x1, blocking collectives, stationary(): normed = lax.all_gather(normed, 'tp', axis=2, tiled=True)  5.96 us
  transfers between devices with their start and end apart: 4, of which 4 were waited for; matrix products, arithmetic and copies ran while one was open for 1% of the time, Pallas kernels for 0%

profile of v1, /device:TPU:2, one launch (start us, length us, event | category | flops | bytes accessed | tf_op | source)
XLA Modules:
  0.0 210.6 jit_solution(6487077089085059324)
XLA Ops:
  6.5 1.2 pad_maximum_fusion
  8.0 16.5 %all_to_all.20 = bf16[16,3,2,8,256]{4,3,2,1,0:T(8,128)(2,1)S(1)} all-to-all(bf16[16,3,2,8,256]{4,3,2,1,0:T(8,128)(2,1)S(1)} %constant_dynamic-update-slice_fusion), channel_id=1, replica_groups=mesh['groups'=2,'tp'=4,'sp'=4] {'sp','tp'}, dimensions={0} | all-to-all | bytes 786432 | tf_op jit(solution)/shard_map/all_to_all | solution.py:131
  25.4 7.9 %all_gather.9 = bf16[2,128,1024]{2,1,0:T(8,128)(2,1)S(1)} all-gather(bf16[2,128,256]{2,1,0:T(8,128)(2,1)S(1)} %copy.67), channel_id=1, replica_groups=mesh['groups'=2,'tp'=4,'sp'=4] {'tp'}, dimensions={2}, use_global_device_ids=true | all-gather | bytes 655360 | tf_op jit(solution)/shard_map/all_gather | solution.py:156
  33.2 1.9 convolution_convert_fusion.2
  35.1 1.1 copy.68
  37.6 34.9 %all-reduce.6.cloned.1.call-done = bf16[2,128,640]{2,0,1:T(2,128)(2,1)} async-done(((bf16[2,128,640]{2,0,1:T(2,128)(2,1)}), bf16[2,128,640]{2,0,1:T(2,128)(2,1)}) %all-reduce.6.cloned.1.call-update) | async-done | bytes 327696
  72.5 0.9 constant_dynamic-slice_fusion.1
  73.5 5.9 %all-reduce.2 = (f32[2,32]{1,0:T(2,128)S(1)}, f32[2,32]{1,0:T(2,128)S(1)}) all-reduce(f32[2,32]{1,0:T(2,128)S(1)} %get-tuple-element.6, f32[2,32]{1,0:T(2,128)S(1)} %get-tuple-element.5), channel_id=1, replica_groups=mesh['groups'=2,'tp'=4,'sp'=4] {'tp'}, use_global_device_ids=true, to_apply=%region_6.0 | all-reduce | flops 128 | bytes 1024 | tf_op jit(solution)/shard_map/psum | solution.py:162
  79.6 6.0 %all_gather.10 = bf16[2,32,2560]{2,1,0:T(8,128)(2,1)S(1)} all-gather(bf16[2,32,640]{2,1,0:T(8,128)(2,1)S(1)} %add_convert_fusion.1), channel_id=1, replica_groups=mesh['groups'=2,'tp'=4,'sp'=4] {'tp'}, dimensions={2}, use_global_device_ids=true | all-gather | bytes 409600 | tf_op jit(solution)/shard_map/all_gather | solution.py:169
  85.5 2.2 %copy.70 = bf16[2,32,2560]{1,0,2:T(2,128)(2,1)} copy(bf16[2,32,2560]{2,1,0:T(8,128)(2,1)S(1)} %all_gather.10) | data formatting | bytes 655360 | tf_op jit(solution)/shard_map/all_gather | solution.py:169
  87.7 3.7 %reshape.61 = bf16[4,2,20480]{2,1,0:T(2,128)(2,1)S(1)} reshape(bf16[2560,2,32]{2,1,0:T(2,128)(2,1)} %bitcast.100) | data formatting | bytes 655360
  91.4 14.0 %all_to_all.21 = bf16[4,2,20480]{2,1,0:T(2,128)(2,1)S(1)} all-to-all(bf16[4,2,20480]{2,1,0:T(2,128)(2,1)S(1)} %reshape.61), channel_id=1, replica_groups=mesh['groups'=2,'tp'=4,'sp'=4] {'sp'}, dimensions={0} | all-to-all | bytes 655360 | tf_op jit(solution)/shard_map/all_to_all | solution.py:170
  105.4 1.7 reshape.62
  107.1 3.5 %copy.76 = bf16[2,32,4,640]{3,2,1,0:T(4,128)(2,1)S(1)} copy(bf16[2,32,4,640]{1,0,3,2:T(2,128)(2,1)} %bitcast.101) | data formatting | bytes 655360 | tf_op jit(solution)/shard_map/all_to_all | solution.py:170
  110.7 1.8 convolution_convert_fusion
  112.6 24.5 %reduce-scatter.2.cloned.1.call-done = bf16[2,32,1792]{2,1,0:T(8,128)(2,1)} async-done(((bf16[2,128,1792]{2,1,0:T(8,128)(2,1)}), bf16[2,32,1792]{2,1,0:T(8,128)(2,1)}) %reduce-scatter.2.cloned.1.call-update) | async-done | bytes 229392 | tf_op jit(solution)/shard_map/reduce_scatter | solution.py:173
  137.1 1.1 fusion.7
  138.2 18.9 %all_gather.11 = bf16[2,128,1792]{2,1,0:T(8,128)(2,1)S(1)} all-gather(bf16[2,32,1792]{2,1,0:T(8,128)(2,1)S(1)} %fusion.7), channel_id=1, replica_groups=mesh['groups'=2,'tp'=4,'sp'=4] {'sp'}, dimensions={1}, use_global_device_ids=true | all-gather | bytes 1146880 | tf_op jit(solution)/shard_map/all_gather | solution.py:175
  157.1 2.6 %convolution_convert_fusion.1 = bf16[256,640]{1,0:T(8,128)(2,1)S(1)} fusion(bf16[256,1792]{1,0:T(8,128)(2,1)S(1)} %bitcast.106, bf16[640,1792]{1,0:T(8,128)(2,1)} %param.15), kind=kOutput, calls=%fused_computation.1 | convolution fusion | flops 587366400 | bytes 3538944 | tf_op jit(solution)/shard_map/dot_general | solution.py:12
  159.7 1.1 copy.73
  162.0 30.0 %all-reduce.8.cloned.1.call-done = bf16[2,128,640]{2,0,1:T(2,128)(2,1)} async-done(((bf16[2,128,640]{2,0,1:T(2,128)(2,1)}), bf16[2,128,640]{2,0,1:T(2,128)(2,1)}) %all-reduce.8.cloned.1.call-update) | async-done | bytes 327696
  192.0 0.9 constant_dynamic-slice_fusion
  193.0 5.8 %collective-permute-start = (bf16[2,32,640]{2,1,0:T(8,128)(2,1)S(1)}, bf16[2,32,640]{2,1,0:T(8,128)(2,1)S(1)}, u32[]{:S(2)}, u32[]{:S(2)}) collective-permute-start(bf16[2,32,640]{2,1,0:T(8,128)(2,1)S(1)} %copy.74), channel_id=1, source_target_pairs={{0,0},{1,4},{2,8},{3,12},{4,1},{5,5},{6,9},{7,13},{8,2},{9,6},{10,... | collective-permute-start | bytes 245768 | tf_op jit(solution)/shard_map/ppermute | solution.py:181
  198.7 4.7 %collective-permute-done = bf16[2,32,640]{2,1,0:T(8,128)(2,1)S(1)} collective-permute-done((bf16[2,32,640]{2,1,0:T(8,128)(2,1)S(1)}, bf16[2,32,640]{2,1,0:T(8,128)(2,1)S(1)}, u32[]{:S(2)}, u32[]{:S(2)}) %collective-permute-start) | collective-permute-done | bytes 81952 | tf_op jit(solution)/shard_map/ppermute | solution.py:181
  (52 shorter events, 3.2 us)
Async XLA Ops:
  6.5 104.2 %copy-start = (bf16[640,1792]{1,0:T(8,128)(2,1)S(1)}, bf16[640,1792]{1,0:T(8,128)(2,1)}, u32[]{:S(2)}) copy-start(bf16[640,1792]{1,0:T(8,128)(2,1)} %param.14) | copy-start | bytes 6881284
  6.5 65.9 %all-reduce.6.cloned.1.call-start = ((), (), s32[]{:S(2)}) async-start(), calls=%async_computation.4 | async-start | bytes 655360
  25.2 11.1 %copy-start.4 = (u32[32]{0:T(128)S(1)}, u32[32]{0:T(128)}, u32[]{:S(2)}) copy-start(u32[32]{0:T(128)} %constant.26) | copy-start | bytes 388
  25.2 12.3 %copy-start.2 = (f32[4,640]{1,0:T(4,128)S(1)}, f32[4,640]{1,0:T(4,128)}, u32[]{:S(2)}) copy-start(f32[4,640]{1,0:T(4,128)} %param.12) | copy-start | bytes 30724
  25.2 48.2 %copy-start.1 = (bf16[2,32,640]{2,1,0:T(8,128)(2,1)S(1)}, bf16[2,32,640]{2,1,0:T(8,128)(2,1)}, u32[]{:S(2)}) copy-start(bf16[2,32,640]{2,1,0:T(8,128)(2,1)} %param.11) | copy-start | bytes 245764
  36.2 100.8 %reduce-scatter.2.cloned.1.call-start = ((), (), s32[]{:S(2)}) async-start(), calls=%async_computation.3 | async-start | bytes 1146880 | tf_op jit(solution)/shard_map/reduce_scatter | solution.py:173
  112.5 79.4 %all-reduce.8.cloned.1.call-start = ((), (), s32[]{:S(2)}) async-start(), calls=%async_computation.5 | async-start | bytes 655360
  157.1 3.7 %copy-start.3 = (u32[32]{0:T(128)S(1)}, u32[32]{0:T(128)}, u32[]{:S(2)}) copy-start(u32[32]{0:T(128)} %constant.30) | copy-start | bytes 388
  193.0 10.5 %collective-permute-start = (bf16[2,32,640]{2,1,0:T(8,128)(2,1)S(1)}, bf16[2,32,640]{2,1,0:T(8,128)(2,1)S(1)}, u32[]{:S(2)}, u32[]{:S(2)}) collective-permute-start(bf16[2,32,640]{2,1,0:T(8,128)(2,1)S(1)} %copy.74), channel_id=1, source_target_pairs={{0,0},{1,4},{2,8},{3,12},{4,1},{5,5},{6,9},{7,13},{8,2},{9,6},{10,... | collective-permute-start | bytes 245768 | tf_op jit(solution)/shard_map/ppermute | solution.py:181
Sparse Core Ops, SparseCore 0:
  36.4 36.0 all-reduce.5
  112.7 24.3 reduce-scatter.1
  160.9 31.0 all-reduce.7
